TPU v7x, 32 devices: a whole 2x2x4 slice. The times are simulated.
32 devices in a mesh: bank: 4 (over x, core), lane: 8 (over z, y).
Axes of the slice: x: 2, y: 2, z: 4, core: 2. Of those that a mesh axis runs over, the one named last changes fastest.
Arguments:
- amplitudes: float32 [2, 256, 128, 128], P(None, ('bank', 'lane')), may hold values from -6 to 6
- energies: float32 [256, 128, 128], P(('bank', 'lane')), may hold values from -2 to 2
- diagonal_angles: float32 [2, 128], replicated, may hold values from 0.3 to 1.2
Outputs:
- final_parts: float32 [2, 256, 128, 128], P(None, ('bank', 'lane'))
- marginal: float32 [64, 128, 128], P('lane', 'bank')
All inputs are finite; a program needn't handle non-finite values.
Results may differ from a plain program's by a relative error of at most 0.0003.
Values sent between devices are 32-bit elements; how exact they have to be, the bound alone decides.
A program may use at most 64 MiB of HBM per device.

v0:
```python
import jax
import jax.numpy as jnp
from jax import lax
from jax.sharding import PartitionSpec as P

LAYERS = 2


def count_bits(values, count):
    places = jnp.arange(count.bit_length() - 1, dtype=jnp.int32)
    return jnp.sum(values[..., None] >> places & 1, axis=-1)


def walsh_table(count):
    rank = jnp.arange(count, dtype=jnp.int32)
    parity = count_bits(rank[:, None] & rank[None, :], count) % 2
    real_part = jnp.where(parity == 1, -1.0, 1.0).astype(jnp.float32) * count ** (-0.5)
    return real_part


def apply_along(values, dim):
    real_part = walsh_table(values.shape[dim])
    moved = jnp.tensordot(values, real_part, axes=([dim], [0]), precision=lax.Precision.HIGHEST)
    return jnp.moveaxis(moved, -1, dim)


def diagonal_step(values, levels, angle):
    turn = angle * levels
    return jnp.stack(
        [
            values[0] * jnp.cos(turn) + values[1] * jnp.sin(turn),
            values[1] * jnp.cos(turn) - values[0] * jnp.sin(turn),
        ]
    )


def shards(amplitudes, energies, diagonal_angles):
    values = amplitudes
    for layer in range(LAYERS):
        values = diagonal_step(values, energies, diagonal_angles[layer])
        values = apply_along(values, 3)
        values = apply_along(values, 2)
        moved = lax.all_to_all(values, "bank", split_axis=2, concat_axis=1, tiled=True)
        moved = apply_along(moved, 1)
        values = lax.all_to_all(moved, "bank", split_axis=1, concat_axis=2, tiled=True)
        moved = lax.all_to_all(values, "lane", split_axis=3, concat_axis=1, tiled=True)
        spread = moved.reshape(2, lax.axis_size("lane"), -1, moved.shape[2], moved.shape[3])
        moved = apply_along(spread, 1).reshape(moved.shape)
        values = lax.all_to_all(moved, "lane", split_axis=1, concat_axis=3, tiled=True)
    chance = values[0] * values[0] + values[1] * values[1]
    marginal = lax.psum_scatter(chance, "bank", scatter_dimension=1, tiled=True) / lax.axis_size(
        "bank"
    )
    return (values, marginal)


def solution(mesh):
    return jax.shard_map(
        shards,
        mesh=mesh,
        in_specs=(P(None, ("bank", "lane"), None, None), P(("bank", "lane"), None, None), P()),
        out_specs=(P(None, ("bank", "lane"), None, None), P("lane", "bank", None)),
        check_vma=False,
    )
```

profile of v0, /device:TPU:1, one launch (start us, length us, event | category | flops | bytes accessed | tf_op | source)
XLA Modules:
  0.0 247.1 jit_solution(2125116720552454207)
XLA Ops:
  7.3 0.6 copy-done.1
  7.9 3.1 %fusion.18 = (f32[1,8,128,128]{3,2,1,0:T(8,128)S(1)}, f32[1,8,128,128]{3,2,1,0:T(8,128)S(1)}) fusion(f32[2,8,128,128]{3,2,1,0:T(8,128)} %param.3, f32[8,128,128]{2,1,0:T(8,128)} %param.4, f32[128]{0:T(128)S(1)} %get-tuple-element.17), kind=kLoop, calls=%fused_computation.28 | loop fusion | flops 917504 | bytes 2621952 | tf_op jit(solution)/shard_map/stack | solution.py:29
  11.0 1.1 fusion
  12.1 1.0 convolution_bitcast_fusion.5
  13.1 1.4 copy.97
  14.5 4.3 %all-to-all-start = ((f32[2,8,128,128]{3,1,0,2:T(8,128)}), f32[2,8,128,128]{3,1,0,2:T(8,128)S(1)}, u32[]{:S(2)}, u32[]{:S(2)}) async-start(f32[2,8,128,128]{3,1,0,2:T(8,128)} %copy.97), calls=%async_computation | async-start | bytes 2097152 | tf_op jit(solution)/shard_map/all_to_all | solution.py:43
  18.7 13.2 %all-to-all-done = f32[2,8,128,128]{3,1,0,2:T(8,128)S(1)} async-done(((f32[2,8,128,128]{3,1,0,2:T(8,128)}), f32[2,8,128,128]{3,1,0,2:T(8,128)S(1)}, u32[]{:S(2)}, u32[]{:S(2)}) %all-to-all-start) | async-done | bytes 1048608 | tf_op jit(solution)/shard_map/all_to_all | solution.py:43
  32.0 1.0 convolution_bitcast_fusion.4
  33.0 0.6 copy.101
  33.6 17.0 %all_to_all.135 = f32[2,32,32,128]{3,2,0,1:T(8,128)S(1)} all-to-all(f32[2,32,32,128]{3,2,0,1:T(8,128)S(1)} %copy.101), channel_id=1, replica_groups=mesh['bank'=4,'lane'=8] {'bank'}, dimensions={1} | all-to-all | bytes 2097152 | tf_op jit(solution)/shard_map/all_to_all | solution.py:45
  50.7 1.4 copy.104
  52.1 6.3 %all-to-all-start.2 = ((f32[2,8,128,128]{2,1,0,3:T(8,128)}), f32[2,8,128,128]{2,1,0,3:T(8,128)S(1)}, u32[]{:S(2)}, u32[]{:S(2)}) async-start(f32[2,8,128,128]{2,1,0,3:T(8,128)} %copy.104), calls=%async_computation.2 | async-start | bytes 2097152 | tf_op jit(solution)/shard_map/all_to_all | solution.py:46
  58.4 24.5 %all-to-all-done.2 = f32[2,8,128,128]{2,1,0,3:T(8,128)S(1)} async-done(((f32[2,8,128,128]{2,1,0,3:T(8,128)}), f32[2,8,128,128]{2,1,0,3:T(8,128)S(1)}, u32[]{:S(2)}, u32[]{:S(2)}) %all-to-all-start.2) | async-done | bytes 1048608 | tf_op jit(solution)/shard_map/all_to_all | solution.py:46
  83.0 1.6 convolution_bitcast_fusion.3
  85.0 29.5 %all_to_all.136 = f32[2,64,128,16]{2,3,0,1:T(8,128)S(1)} all-to-all(f32[2,64,128,16]{2,3,0,1:T(8,128)S(1)} %copy.109), channel_id=1, replica_groups=mesh['bank'=4,'lane'=8] {'lane'}, dimensions={1} | all-to-all | bytes 2097152 | tf_op jit(solution)/shard_map/all_to_all | solution.py:49
  115.2 0.8 copy-done
  116.0 2.0 add_bitcast_fusion
  118.0 1.1 fusion.4
  119.1 1.0 convolution_bitcast_fusion.2
  120.6 17.7 %all_to_all.137 = f32[2,8,128,128]{3,1,0,2:T(8,128)S(1)} all-to-all(f32[2,8,128,128]{3,1,0,2:T(8,128)S(1)} %copy.118), channel_id=1, replica_groups=mesh['bank'=4,'lane'=8] {'bank'}, dimensions={2} | all-to-all | bytes 2097152 | tf_op jit(solution)/shard_map/all_to_all | solution.py:43
  138.3 1.0 convolution_bitcast_fusion.1
  139.4 0.6 copy.122
  140.0 16.9 %all_to_all.138 = f32[2,32,32,128]{3,2,0,1:T(8,128)S(1)} all-to-all(f32[2,32,32,128]{3,2,0,1:T(8,128)S(1)} %copy.122), channel_id=1, replica_groups=mesh['bank'=4,'lane'=8] {'bank'}, dimensions={1} | all-to-all | bytes 2097152 | tf_op jit(solution)/shard_map/all_to_all | solution.py:45
  156.9 0.5 copy.125
  157.5 28.1 %all_to_all.139 = f32[2,8,128,128]{2,1,0,3:T(8,128)S(1)} all-to-all(f32[2,8,128,128]{2,1,0,3:T(8,128)S(1)} %copy.125), channel_id=1, replica_groups=mesh['bank'=4,'lane'=8] {'lane'}, dimensions={3} | all-to-all | bytes 2097152 | tf_op jit(solution)/shard_map/all_to_all | solution.py:46
  185.6 1.6 convolution_bitcast_fusion
  187.6 28.7 %all_to_all.140 = f32[2,64,128,16]{2,3,0,1:T(8,128)S(1)} all-to-all(f32[2,64,128,16]{2,3,0,1:T(8,128)S(1)} %copy.130), channel_id=1, replica_groups=mesh['bank'=4,'lane'=8] {'lane'}, dimensions={1} | all-to-all | bytes 2097152 | tf_op jit(solution)/shard_map/all_to_all | solution.py:49
  216.5 1.0 copy.134
  217.6 1.3 copy.135
  218.9 19.7 %reduce-scatter.2.cloned.1.call-done = f32[8,32,128]{2,0,1:T(8,128)} async-done(((f32[8,128,128]{2,0,1:T(8,128)}), f32[8,32,128]{2,0,1:T(8,128)}) %reduce-scatter.2.cloned.1.call-update) | async-done | bytes 131088 | tf_op jit(solution)/shard_map/reduce_scatter | solution.py:51
  238.6 0.9 broadcast_multiply_fusion
  239.6 0.7 copy.136
  (29 shorter events, 2.5 us)
Async XLA Ops:
  7.2 0.7 copy-start.1
  14.5 17.5 %all-to-all-start = ((f32[2,8,128,128]{3,1,0,2:T(8,128)}), f32[2,8,128,128]{3,1,0,2:T(8,128)S(1)}, u32[]{:S(2)}, u32[]{:S(2)}) async-start(f32[2,8,128,128]{3,1,0,2:T(8,128)} %copy.97), calls=%async_computation | async-start | bytes 2097152 | tf_op jit(solution)/shard_map/all_to_all | solution.py:43
  52.1 30.9 %all-to-all-start.2 = ((f32[2,8,128,128]{2,1,0,3:T(8,128)}), f32[2,8,128,128]{2,1,0,3:T(8,128)S(1)}, u32[]{:S(2)}, u32[]{:S(2)}) async-start(f32[2,8,128,128]{2,1,0,3:T(8,128)} %copy.104), calls=%async_computation.2 | async-start | bytes 2097152 | tf_op jit(solution)/shard_map/all_to_all | solution.py:46
  58.4 180.3 %reduce-scatter.2.cloned.1.call-start = ((), (), s32[]{:S(2)}) async-start(), calls=%async_computation.9 | async-start | bytes 655360 | tf_op jit(solution)/shard_map/reduce_scatter | solution.py:51
  114.9 1.0 copy-start
Sparse Core Ops, SparseCore 0:
  217.6 20.9 reduce-scatter.1
where the time goes:
time: 248 us; the launch traced here: 247 us
  blocking collectives  138 us (56%)
  waiting for transfers between devices  57.5 us (23%)
  between operations  14.3 us (6%)
  local copies, waits for them, and re-layouts  11.1 us (4%)
  starting transfers between devices  10.6 us (4%)
  matrix products  9.46 us (4%)
  other arithmetic  6.2 us (2%)
    all_to_all x2, blocking collectives, shards(): lax.all_to_all(moved, 'lane', split_axis=1, concat_axis=3, tiled=True)  58.2 us
    all_to_all x2, blocking collectives, shards(): lax.all_to_all(moved, 'bank', split_axis=1, concat_axis=2, tiled=True)  33.8 us
    all_to_all x1, blocking collectives, shards(): lax.all_to_all(values, 'lane', split_axis=3, concat_axis=1, tiled=True)  28.1 us
    all_to_all x1, waiting for transfers between devices, shards(): lax.all_to_all(values, 'lane', split_axis=3, concat_axis=1, tiled=True)  24.5 us
    reduce_scatter x1, waiting for transfers between devices, shards(): lax.psum_scatter(chance, 'bank', scatter_dimension=1, tiled=True)  19.7 us
    all_to_all x1, blocking collectives, shards(): lax.all_to_all(values, 'bank', split_axis=2, concat_axis=1, tiled=True)  17.7 us
    all_to_all x1, waiting for transfers between devices, shards(): lax.all_to_all(values, 'bank', split_axis=2, concat_axis=1, tiled=True)  13.2 us
    dot_general x8, matrix products, apply_along(): jnp.tensordot(values, real_part, axes=([dim], [0]), precision=lax.Precisi...  9.46 us
  transfers between devices with their start and end apart: 3, of which 3 were waited for; matrix products, arithmetic and copies ran while one was open for 1% of the time, Pallas kernels for 0%

commit v1 on v0

v1 whole, which is shorter than its diff:
```python
import functools

import jax
import jax.numpy as jnp
import numpy as np
from jax import lax
from jax.experimental import pallas as pl
from jax.experimental.pallas import tpu as pltpu
from jax.sharding import PartitionSpec as P

MESH = pl.DeviceIdType.MESH
TABLE = 256
SUB = 8
CHUNKS = 4


def walsh_table():
    rank = np.arange(TABLE)
    both = rank[:, None] & rank[None, :]
    parity = sum((both >> place) & 1 for place in range(8)) % 2
    return jnp.asarray(np.where(parity == 1, -1.0, 1.0) / 16.0, jnp.bfloat16)


def cos_sin(turn):
    half = turn * 0.5
    x = half * half
    s = -1.0 / 39916800.0
    for term in (1.0 / 362880.0, -1.0 / 5040.0, 1.0 / 120.0, -1.0 / 6.0, 1.0):
        s = s * x + term
    s = s * half
    c = 1.0 / 479001600.0
    for term in (-1.0 / 3628800.0, 1.0 / 40320.0, -1.0 / 720.0, 1.0 / 24.0, -0.5, 1.0):
        c = c * x + term
    return 1.0 - 2.0 * (s * s), 2.0 * (s * c)


def split(values):
    high = values.astype(jnp.bfloat16)
    return high, (values - high.astype(jnp.float32)).astype(jnp.bfloat16)


def mix(items):
    items, step = list(items), 1
    while step < len(items):
        for low in range(len(items)):
            if not low & step:
                u, v = items[low], items[low + step]
                items[low], items[low + step] = u + v, u - v
        step *= 2
    return items


def dot(a, b):
    return jnp.dot(a, b, preferred_element_type=jnp.float32)


def mix_lanes(values, table):
    high, low = split(values)
    return dot(jnp.concatenate([high, low], axis=1), table[:, :128])


def kernel(
    n_bank, n_lane, chunks,
    a_ref, e_ref, angle_ref, table_ref,
    out_ref, marginal_ref,
    held, sent1, got1, sent2, got2, levels, cosine, sine, chance, chances,
    e_send, e_recv, send1, recv1, send2, recv2, m_send, m_recv,
):
    devices = n_bank * n_lane
    _, blocks, rows, lanes = a_ref.shape
    group = blocks * rows // devices
    piece = group // chunks
    groups = rows // group
    tiles = piece // SUB
    bank, lane = lax.axis_index("bank"), lax.axis_index("lane")
    me = bank * n_lane + lane

    def place(device):
        return (device // n_lane, device % n_lane)

    barrier = pltpu.get_barrier_semaphore()

    def greet(step, _):
        pl.semaphore_signal(
            barrier, inc=1, device_id=place((me + step) % devices), device_id_type=MESH
        )
        return 0

    lax.fori_loop(1, devices, greet, 0)
    pl.semaphore_wait(barrier, devices - 1)

    def swap(src, dst, send_sem, recv_sem):
        def one(step, _):
            other = (me + step) % devices
            pltpu.make_async_remote_copy(
                src_ref=src.at[other], dst_ref=dst.at[me],
                send_sem=send_sem, recv_sem=recv_sem,
                device_id=place(other), device_id_type=MESH,
            ).start()
            return 0

        lax.fori_loop(1, devices, one, 0)

    def arrive(buffer, sem):
        most = buffer.at[pl.ds(0, devices - 1)]
        pltpu.make_async_copy(most, most, sem).wait()

    swap(e_ref, levels, e_send, e_recv)
    levels[me] = e_ref[me]

    table = table_ref[...]

    def block_step(b, _):
        first = b * groups
        level = e_ref[pl.ds(first, groups)].reshape(rows, lanes)
        c, s = cos_sin(level * angle_ref[0:1, :])
        re, im = a_ref[0, b], a_ref[1, b]
        turned = jnp.concatenate([re * c + im * s, im * c - re * s], axis=0)
        along = mix_lanes(turned, table)
        high, low = split(jnp.concatenate([along[:rows], along[rows:]], axis=1))
        mixed = dot(table[:128, :], jnp.concatenate([high, low], axis=0))
        held[b, 0] = mixed[:, :lanes]
        held[b, 1] = mixed[:, lanes:]
        return 0

    lax.fori_loop(0, blocks, block_step, 0)

    for chunk in range(chunks):
        def spread(g, _, chunk=chunk):
            start = pl.multiple_of(g * group + chunk * piece, SUB)
            for part in range(2):
                mixed = mix([held[b, part, pl.ds(start, piece), :] for b in range(blocks)])
                for b in range(blocks):
                    sent1[chunk, b * groups + g, part] = mixed[b]
            return 0

        lax.fori_loop(0, groups, spread, 0)
        swap(sent1.at[chunk], got1.at[chunk], send1.at[chunk], recv1.at[chunk])
        got1[chunk, me] = sent1[chunk, me]

    arrive(levels, e_recv)

    def phases(d, _):
        c, s = cos_sin(levels[d] * angle_ref[1:2, :])
        cosine[d] = c
        sine[d] = s
        return 0

    lax.fori_loop(0, devices, phases, 0)

    wide = TABLE // SUB
    for chunk in range(chunks):
        arrive(got1.at[chunk], recv1.at[chunk])
        for tile in range(tiles):
            here = pl.ds(tile * SUB, SUB)
            there = pl.ds(chunk * piece + tile * SUB, SUB)
            re = mix([got1[chunk, d, 0, here, :] for d in range(devices)])
            im = mix([got1[chunk, d, 1, here, :] for d in range(devices)])
            done = []
            for start in range(0, devices, wide):
                span = range(start, start + wide)
                r, i = [], []
                for d in span:
                    c, s = cosine[d, there, :], sine[d, there, :]
                    r.append(re[d] * c + im[d] * s)
                    i.append(im[d] * c - re[d] * s)
                along = mix_lanes(jnp.concatenate(r + i, axis=0), table)
                pair = jnp.concatenate([along[:TABLE], along[TABLE:]], axis=1)
                high, low = split(pair)
                done.append(dot(table, high) + dot(table, low))
            done = mix(done)
            for d in range(devices):
                at = d % wide * SUB
                tile_of = done[d // wide][at : at + SUB]
                sent2[chunk, d, 0, here, :] = tile_of[:, :lanes]
                sent2[chunk, d, 1, here, :] = tile_of[:, lanes:]
        swap(sent2.at[chunk], got2.at[chunk], send2.at[chunk], recv2.at[chunk])
        got2[chunk, me] = sent2[chunk, me]

    for chunk in range(chunks):
        arrive(got2.at[chunk], recv2.at[chunk])
        for tile in range(tiles):
            here = pl.ds(tile * SUB, SUB)
            for part in range(2):
                mixed = mix([got2[chunk, d, part, here, :] for d in range(devices)])
                for d in range(devices):
                    got2[chunk, d, part, here, :] = mixed[d]

    scale = float(TABLE * TABLE) / (devices * blocks * rows * lanes)
    strip = rows // n_bank

    def finish(d, _):
        b, row = d // groups, d % groups * group
        both = []
        for part in range(2):
            both.append(mix([
                got2[chunk, d, part, tile * SUB : (tile + 1) * SUB, :]
                for chunk in range(chunks) for tile in range(tiles)
            ]))
        for place_, (r, i) in enumerate(zip(*both)):
            r, i = r * scale, i * scale
            at = row + place_ * SUB
            out_ref[0, b, pl.ds(pl.multiple_of(at, SUB), SUB), :] = r
            out_ref[1, b, pl.ds(pl.multiple_of(at, SUB), SUB), :] = i
            chance[at // strip, b, pl.ds(pl.multiple_of(at % strip, SUB), SUB), :] = r * r + i * i
        return 0

    lax.fori_loop(0, devices, finish, 0)

    copies = []
    for step in range(1, n_bank):
        other = (bank + step) % n_bank
        copies.append(pltpu.make_async_remote_copy(
            src_ref=chance.at[other], dst_ref=chances.at[step - 1],
            send_sem=m_send.at[step - 1], recv_sem=m_recv.at[step - 1],
            device_id=(other, lane), device_id_type=MESH,
        ))
        copies[-1].start()
    for copy in copies:
        copy.wait()
    total = chance[bank]
    for step in range(1, n_bank):
        total = total + chances[step - 1]
    marginal_ref[...] = total * (1.0 / n_bank)

    arrive(e_ref, e_send)
    for chunk in range(chunks):
        arrive(sent1.at[chunk], send1.at[chunk])
        arrive(sent2.at[chunk], send2.at[chunk])


def shards(n_bank, n_lane, amplitudes, energies, angles):
    devices = n_bank * n_lane
    _, blocks, rows, lanes = amplitudes.shape
    group = blocks * rows // devices
    chunks = min(CHUNKS, group // SUB)
    piece = group // chunks
    f32 = jnp.float32
    whole = pl.BlockSpec(memory_space=pltpu.VMEM)
    swapped = pltpu.VMEM((chunks, devices, 2, piece, lanes), f32)
    real = pltpu.VMEM((devices, group, lanes), f32)
    strip = (blocks, rows // n_bank, lanes)
    one, many = pltpu.SemaphoreType.DMA, pltpu.SemaphoreType.DMA((chunks,))
    return pl.pallas_call(
        functools.partial(kernel, n_bank, n_lane, chunks),
        out_shape=(
            jax.ShapeDtypeStruct(amplitudes.shape, f32),
            jax.ShapeDtypeStruct(strip, f32),
        ),
        in_specs=[whole] * 4,
        out_specs=(whole, whole),
        scratch_shapes=[
            pltpu.VMEM((blocks, 2, rows, lanes), f32),
            swapped, swapped, swapped, swapped,
            real, real, real,
            pltpu.VMEM((n_bank, *strip), f32),
            pltpu.VMEM((n_bank - 1, *strip), f32),
            one, one, many, many, many, many,
            pltpu.SemaphoreType.DMA((n_bank - 1,)),
            pltpu.SemaphoreType.DMA((n_bank - 1,)),
        ],
        compiler_params=pltpu.CompilerParams(collective_id=0, has_side_effects=True),
        name="walsh",
    )(amplitudes, energies.reshape(devices, group, lanes), angles, walsh_table())


def solution(mesh):
    sizes = mesh.shape
    return jax.shard_map(
        functools.partial(shards, sizes["bank"], sizes["lane"]),
        mesh=mesh,
        in_specs=(P(None, ("bank", "lane"), None, None), P(("bank", "lane"), None, None), P()),
        out_specs=(P(None, ("bank", "lane"), None, None), P("lane", "bank", None)),
        check_vma=False,
    )
```

time: 248 us -> 78.6 us (0.32)
  blocking collectives: 138 us -> 0 us
  Pallas kernels: 0 us -> 74.8 us
  waiting for transfers between devices: 57.5 us -> 0 us
  between operations: 14.3 us -> 0.65 us
  starting transfers between devices: 10.6 us -> 0 us
  matrix products: 9.46 us -> 0 us
  local copies, waits for them, and re-layouts: 11.1 us -> 2.99 us
  other arithmetic: 6.2 us -> 0 us
    all_to_all x6 -> x0, blocking collectives: 138 us -> none  [the longest x2 58.2 us: shards(): lax.all_to_all(moved, 'lane', split_axis=1, concat_axis=3, tiled=True)]
    pallas_call x0 -> x1, Pallas kernels: none -> 74.8 us  [shards(): pl.pallas_call(functools.partial(kernel, n_bank, n_lane, chunks), out_sha...]
    all_to_all x2 -> x0, waiting for transfers between devices: 37.8 us -> none  [the longest x1 24.5 us: shards(): lax.all_to_all(values, 'lane', split_axis=3, concat_axis=1, tiled=True)]
    reduce_scatter x1 -> x0, waiting for transfers between devices: 19.7 us -> none  [shards(): lax.psum_scatter(chance, 'bank', scatter_dimension=1, tiled=True)]
    all_to_all x2 -> x0, starting transfers between devices: 10.5 us -> none  [the longest x1 6.28 us: shards(): lax.all_to_all(values, 'lane', split_axis=3, concat_axis=1, tiled=True)]
    dot_general x8 -> x0, matrix products: 9.46 us -> none  [apply_along(): jnp.tensordot(values, real_part, axes=([dim], [0]), precision=lax.Precisi...]
    another operation x2 -> x0, other arithmetic: 5.08 us -> none  [diagonal_step(): jnp.stack([values[0] * jnp.cos(turn) + values[1] * jnp.sin(turn), values[...]
    transpose x6 -> x0, local copies, waits for them, and re-layouts: 3.52 us -> none  [apply_along(): return jnp.moveaxis(moved, -1, dim)]
  transfers between devices with their start and end apart: 3 -> 0, of which waited for: 3 -> 0; matrix products, arithmetic and copies ran while one was open for 1% -> 0% of each run, Pallas kernels for 0% -> 0%
where the time goes in v1:
time: 78.6 us; the launch traced here: 78.4 us
  Pallas kernels  74.8 us (95%)
  local copies, waits for them, and re-layouts  2.99 us (4%)
    pallas_call x1, Pallas kernels, shards(): pl.pallas_call(functools.partial(kernel, n_bank, n_lane, chunks), out_sha...  74.8 us
    unnamed x4, local copies, waits for them, and re-layouts  2.99 us

profile of v1, /device:TPU:1, one launch (start us, length us, event | category | flops | bytes accessed | tf_op | source)
XLA Modules:
  0.0 78.4 jit_solution(13890390295566057023)
XLA Ops:
  0.6 74.8 %walsh.1 = (f32[2,8,128,128]{3,2,1,0:T(8,128)}, f32[8,32,128]{2,1,0:T(8,128)}) custom-call(f32[2,8,128,128]{3,2,1,0:T(8,128)} %a_ref.1, f32[32,32,128]{2,1,0:T(8,128)} %bitcast.1, f32[2,128]{1,0:T(2,128)} %angle_ref.1, bf16[256,256]{1,0:T(8,128)(2,1)} %constant.2.clone.table_ref), custom_call_target="tpu_custom_call" | custom-call | tf_op jit(solution)/shard_map/walsh/pallas_call | solution.py:244
  75.4 0.0 copy-start
  75.4 2.3 %copy.8 = f32[2,8,128,128]{3,2,1,0:T(8,128)} copy(f32[2,8,128,128]{3,2,1,0:T(8,128)} %get-tuple-element.4) | data formatting | bytes 2097152
  77.7 0.0 copy-done
  77.7 0.7 copy.9
Async XLA Ops:
  75.4 2.3 %copy-start = (f32[8,32,128]{2,1,0:T(8,128)S(1)}, f32[8,32,128]{2,1,0:T(8,128)}, u32[]{:S(2)}) copy-start(f32[8,32,128]{2,1,0:T(8,128)} %get-tuple-element.5) | copy-start | bytes 393220

commit v2 on v1

v2 whole, which is shorter than its diff:
```python
import functools

import jax
import jax.numpy as jnp
import numpy as np
from jax import lax
from jax.experimental import pallas as pl
from jax.experimental.pallas import tpu as pltpu
from jax.sharding import PartitionSpec as P

MESH = pl.DeviceIdType.MESH
TABLE = 256
SUB = 8


def walsh_table():
    rank = np.arange(TABLE)
    both = rank[:, None] & rank[None, :]
    parity = sum((both >> place) & 1 for place in range(8)) % 2
    return jnp.asarray(np.where(parity == 1, -1.0, 1.0) / 16.0, jnp.bfloat16)


def cos_sin(turn):
    half = turn * 0.5
    x = half * half
    s = -1.0 / 39916800.0
    for term in (1.0 / 362880.0, -1.0 / 5040.0, 1.0 / 120.0, -1.0 / 6.0, 1.0):
        s = s * x + term
    s = s * half
    c = 1.0 / 479001600.0
    for term in (-1.0 / 3628800.0, 1.0 / 40320.0, -1.0 / 720.0, 1.0 / 24.0, -0.5, 1.0):
        c = c * x + term
    return 1.0 - 2.0 * (s * s), 2.0 * (s * c)


def split(values):
    high = values.astype(jnp.bfloat16)
    return high, (values - high.astype(jnp.float32)).astype(jnp.bfloat16)


def mix(items):
    items, step = list(items), 1
    while step < len(items):
        for low in range(len(items)):
            if not low & step:
                u, v = items[low], items[low + step]
                items[low], items[low + step] = u + v, u - v
        step *= 2
    return items


def dot(a, b):
    return jnp.dot(a, b, preferred_element_type=jnp.float32)


def mix_lanes(values, table):
    high, low = split(values)
    return dot(jnp.concatenate([high, low], axis=1), table[:, :128])


def kernel(
    n_bank, n_lane, chunks,
    a_hbm, e_hbm, angle_hbm, table_hbm,
    out_ref, marginal_ref,
    a_ref, e_ref, angle_ref, table_ref,
    held, sent1, got1, sent2, got2, levels, cosine, sine, chance, chances,
    in_sem, e_send, e_recv, send1, recv1, send2, recv2, m_send, m_recv,
):
    devices = n_bank * n_lane
    _, blocks, rows, lanes = a_ref.shape
    group = blocks * rows // devices
    groups = rows // group
    bank, lane = lax.axis_index("bank"), lax.axis_index("lane")
    me = bank * n_lane + lane

    fetches = [
        pltpu.make_async_copy(src, dst, in_sem.at[i])
        for i, (src, dst) in enumerate([
            (e_hbm, e_ref), (a_hbm, a_ref), (angle_hbm, angle_ref), (table_hbm, table_ref),
        ])
    ]
    for fetch in fetches:
        fetch.start()

    def others(act):
        half = n_lane // 2

        def around(step, first_bank):
            there = lax.rem(lane + half + step, n_lane)
            for turn in range(first_bank, n_bank):
                act(lax.rem(bank + turn, n_bank), there)
            return 0

        lax.fori_loop(0, half, lambda step, _: around(step, 0), 0)
        lax.fori_loop(half + 1, n_lane, lambda step, _: around(step, 0), 0)
        around(half, 1)

    barrier = pltpu.get_barrier_semaphore()

    def greet(to_bank, to_lane):
        pl.semaphore_signal(
            barrier, inc=1, device_id=(to_bank, to_lane), device_id_type=MESH
        )

    others(greet)
    fetches[0].wait()
    pl.semaphore_wait(barrier, devices - 1)

    def swap(src, dst, send_sem, recv_sem):
        def one(to_bank, to_lane):
            pltpu.make_async_remote_copy(
                src_ref=src.at[to_bank * n_lane + to_lane], dst_ref=dst.at[me],
                send_sem=send_sem, recv_sem=recv_sem,
                device_id=(to_bank, to_lane), device_id_type=MESH,
            ).start()

        others(one)

    def arrive(buffer, sem):
        most = buffer.at[pl.ds(0, devices - 1)]
        pltpu.make_async_copy(most, most, sem).wait()

    swap(e_ref, levels, e_send, e_recv)
    levels[me] = e_ref[me]
    for fetch in fetches[1:]:
        fetch.wait()

    table = table_ref[...]

    def block_step(b, _):
        first = b * groups
        level = e_ref[pl.ds(first, groups)].reshape(rows, lanes)
        c, s = cos_sin(level * angle_ref[0:1, :])
        re, im = a_ref[0, b], a_ref[1, b]
        turned = jnp.concatenate([re * c + im * s, im * c - re * s], axis=0)
        along = mix_lanes(turned, table)
        high, low = split(jnp.concatenate([along[:rows], along[rows:]], axis=1))
        mixed = dot(table[:128, :], jnp.concatenate([high, low], axis=0))
        held[b, 0] = mixed[:, :lanes]
        held[b, 1] = mixed[:, lanes:]
        return 0

    lax.fori_loop(0, blocks, block_step, 0)

    for chunk in range(chunks):
        def spread(g, _, chunk=chunk):
            start = pl.multiple_of(g * group + chunk * SUB, SUB)
            for part in range(2):
                mixed = mix([held[b, part, pl.ds(start, SUB), :] for b in range(blocks)])
                for b in range(blocks):
                    sent1[chunk, b * groups + g, part] = mixed[b]
            return 0

        lax.fori_loop(0, groups, spread, 0)
        swap(sent1.at[chunk], got1.at[chunk], send1.at[chunk], recv1.at[chunk])
        got1[chunk, me] = sent1[chunk, me]

    arrive(levels, e_recv)

    def phases(d, _):
        c, s = cos_sin(levels[d] * angle_ref[1:2, :])
        cosine[d] = c
        sine[d] = s
        return 0

    lax.fori_loop(0, devices, phases, 0)

    wide = TABLE // SUB
    lag = 2 if chunks > 1 else 1
    for chunk in range(chunks):
        arrive(got1.at[chunk], recv1.at[chunk])
        there = pl.ds(chunk * SUB, SUB)
        re = mix([got1[chunk, d, 0] for d in range(devices)])
        im = mix([got1[chunk, d, 1] for d in range(devices)])
        done = []
        for start in range(0, devices, wide):
            r, i = [], []
            for d in range(start, start + wide):
                c, s = cosine[d, there, :], sine[d, there, :]
                r.append(re[d] * c + im[d] * s)
                i.append(im[d] * c - re[d] * s)
            along = mix_lanes(jnp.concatenate(r + i, axis=0), table)
            pair = jnp.concatenate([along[:TABLE], along[TABLE:]], axis=1)
            high, low = split(pair)
            done.append(dot(table, high) + dot(table, low))
        done = mix(done)
        for d in range(devices):
            at = d % wide * SUB
            for part in range(2):
                tile = done[d // wide][at : at + SUB, part * lanes : (part + 1) * lanes]
                if chunk % lag:
                    before = sent2[chunk - 1, d, part]
                    sent2[chunk - 1, d, part] = before + tile
                    sent2[chunk, d, part] = before - tile
                else:
                    sent2[chunk, d, part] = tile
        if chunk % lag == lag - 1:
            for ready in range(chunk - lag + 1, chunk + 1):
                swap(sent2.at[ready], got2.at[ready], send2.at[ready], recv2.at[ready])
                got2[ready, me] = sent2[ready, me]

    scale = float(TABLE * TABLE) / (devices * blocks * rows * lanes)
    pieces = lag
    layers = chunks // pieces
    share = rows // n_bank // group

    def back(chunk, part):
        return mix([got2[chunk, d, part] for d in range(devices)])

    for chunk in range(chunks - pieces):
        arrive(got2.at[chunk], recv2.at[chunk])
        for part in range(2):
            mixed = back(chunk, part)
            for d in range(devices):
                got2[chunk, d, part] = mixed[d]

    copies = []
    for piece in range(pieces):
        last = chunks - pieces + piece
        arrive(got2.at[last], recv2.at[last])
        for part in range(2):
            mixed = back(last, part)
            for d in range(devices):
                tiles = [got2[t, d, part] for t in range(piece, last, pieces)]
                tiles = mix(tiles + [mixed[d]])
                b, g = divmod(d, groups)
                for t in range(layers):
                    value = tiles[t] * scale
                    at = g * group + (t * pieces + piece) * SUB
                    out_ref[part, b, at : at + SUB, :] = value
                    spot = (piece, g // share, b, pl.ds((g % share * layers + t) * SUB, SUB))
                    square = value * value
                    chance[spot] = chance[spot] + square if part else square
        for step in range(1, n_bank):
            other = lax.rem(bank + step, n_bank)
            copies.append(pltpu.make_async_remote_copy(
                src_ref=chance.at[piece, other], dst_ref=chances.at[piece, step - 1],
                send_sem=m_send.at[piece, step - 1], recv_sem=m_recv.at[piece, step - 1],
                device_id=(other, lane), device_id_type=MESH,
            ))
            copies[-1].start()
    for piece in range(pieces):
        for copy in copies[piece * (n_bank - 1) : (piece + 1) * (n_bank - 1)]:
            copy.wait_recv()
        total = chance[piece, bank]
        for step in range(1, n_bank):
            total = total + chances[piece, step - 1]
        total = total * (1.0 / n_bank)
        for g in range(share):
            for t in range(layers):
                at = g * group + (t * pieces + piece) * SUB
                of = (g * layers + t) * SUB
                marginal_ref[:, at : at + SUB, :] = total[:, of : of + SUB]

    for copy in copies:
        copy.wait_send()
    arrive(e_ref, e_send)
    for chunk in range(chunks):
        arrive(sent1.at[chunk], send1.at[chunk])
        arrive(sent2.at[chunk], send2.at[chunk])


def shards(n_bank, n_lane, amplitudes, energies, angles):
    devices = n_bank * n_lane
    _, blocks, rows, lanes = amplitudes.shape
    group = blocks * rows // devices
    chunks = group // SUB
    pieces = min(2, chunks)
    f32 = jnp.float32
    table = walsh_table()
    whole = pl.BlockSpec(memory_space=pltpu.VMEM)
    swapped = pltpu.VMEM((chunks, devices, 2, SUB, lanes), f32)
    real = pltpu.VMEM((devices, group, lanes), f32)
    strip = (blocks, rows // n_bank, lanes)
    part = (blocks, rows // n_bank // pieces, lanes)
    one, many = pltpu.SemaphoreType.DMA, pltpu.SemaphoreType.DMA((chunks,))
    return pl.pallas_call(
        functools.partial(kernel, n_bank, n_lane, chunks),
        out_shape=(
            pltpu.VMEM(amplitudes.shape, f32),
            pltpu.VMEM(strip, f32),
        ),
        in_specs=[pl.BlockSpec(memory_space=pltpu.HBM)] * 4,
        out_specs=(whole, whole),
        scratch_shapes=[
            pltpu.VMEM(amplitudes.shape, f32),
            real,
            pltpu.VMEM(angles.shape, f32),
            pltpu.VMEM(table.shape, table.dtype),
            pltpu.VMEM((blocks, 2, rows, lanes), f32),
            swapped, swapped, swapped, swapped,
            real, real, real,
            pltpu.VMEM((pieces, n_bank, *part), f32),
            pltpu.VMEM((pieces, n_bank - 1, *part), f32),
            pltpu.SemaphoreType.DMA((4,)),
            one, one, many, many, many, many,
            pltpu.SemaphoreType.DMA((pieces, n_bank - 1)),
            pltpu.SemaphoreType.DMA((pieces, n_bank - 1)),
        ],
        compiler_params=pltpu.CompilerParams(
            collective_id=0, has_side_effects=True
        ),
        name="walsh",
    )(amplitudes, energies.reshape(devices, group, lanes), angles, table)


def solution(mesh):
    sizes = mesh.shape
    return jax.shard_map(
        functools.partial(shards, sizes["bank"], sizes["lane"]),
        mesh=mesh,
        in_specs=(P(None, ("bank", "lane"), None, None), P(("bank", "lane"), None, None), P()),
        out_specs=(P(None, ("bank", "lane"), None, None), P("lane", "bank", None)),
        check_vma=False,
    )
```

time: 78.6 us -> 72.4 us (0.921)
  Pallas kernels: 74.8 us -> 70 us
  local copies, waits for them, and re-layouts: 2.99 us -> 1.63 us
    pallas_call x1, Pallas kernels: 74.8 us -> 70 us  [shards(): pl.pallas_call(functools.partial(kernel, n_bank, n_lane, chunks), out_sha...]
    unnamed x4 -> x2, local copies, waits for them, and re-layouts: 2.99 us -> 1.63 us
where the time goes in v2:
time: 72.4 us; the launch traced here: 72.2 us
  Pallas kernels  70 us (97%)
  local copies, waits for them, and re-layouts  1.63 us (2%)
    pallas_call x1, Pallas kernels, shards(): pl.pallas_call(functools.partial(kernel, n_bank, n_lane, chunks), out_sha...  70 us
    unnamed x2, local copies, waits for them, and re-layouts  1.63 us

profile of v2, /device:TPU:1, one launch (start us, length us, event | category | flops | bytes accessed | tf_op | source)
XLA Modules:
  0.0 72.2 jit_solution(14745113641665240231)
XLA Ops:
  0.6 70.0 %walsh.1 = (f32[2,8,128,128]{3,2,1,0:T(8,128)S(1)}, f32[8,32,128]{2,1,0:T(8,128)S(1)}) custom-call(f32[2,8,128,128]{3,2,1,0:T(8,128)} %a_hbm.1, f32[32,32,128]{2,1,0:T(8,128)} %bitcast.1, f32[2,128]{1,0:T(2,128)} %angle_hbm.1, bf16[256,256]{1,0:T(8,128)(2,1)} %constant.2.clone.table_hbm), custom_call_target="tpu_custom_call" | custom-call | tf_op jit(solution)/shard_map/walsh/pallas_call | solution.py:277
  70.6 1.0 %copy.8 = f32[2,8,128,128]{3,2,1,0:T(8,128)} copy(f32[2,8,128,128]{3,2,1,0:T(8,128)S(1)} %get-tuple-element.2) | data formatting | bytes 2097152
  71.6 0.7 copy.9

commit v3 on v2

--- a/solution.py
+++ b/solution.py
@@ -260,6 +260,17 @@
         arrive(sent2.at[chunk], send2.at[chunk])
 
 
+def put_out(state_ref, marginal_ref, state_out, marginal_out, sem):
+    copies = [
+        pltpu.make_async_copy(state_ref, state_out, sem.at[0]),
+        pltpu.make_async_copy(marginal_ref, marginal_out, sem.at[1]),
+    ]
+    for copy in copies:
+        copy.start()
+    for copy in copies:
+        copy.wait()
+
+
 def shards(n_bank, n_lane, amplitudes, energies, angles):
     devices = n_bank * n_lane
     _, blocks, rows, lanes = amplitudes.shape
@@ -274,7 +285,7 @@
     strip = (blocks, rows // n_bank, lanes)
     part = (blocks, rows // n_bank // pieces, lanes)
     one, many = pltpu.SemaphoreType.DMA, pltpu.SemaphoreType.DMA((chunks,))
-    return pl.pallas_call(
+    state, marginal = pl.pallas_call(
         functools.partial(kernel, n_bank, n_lane, chunks),
         out_shape=(
             pltpu.VMEM(amplitudes.shape, f32),
@@ -302,6 +313,18 @@
         ),
         name="walsh",
     )(amplitudes, energies.reshape(devices, group, lanes), angles, table)
+    return pl.pallas_call(
+        put_out,
+        out_shape=(
+            jax.ShapeDtypeStruct(state.shape, f32),
+            jax.ShapeDtypeStruct(marginal.shape, f32),
+        ),
+        in_specs=[whole] * 2,
+        out_specs=(pl.BlockSpec(memory_space=pltpu.HBM),) * 2,
+        scratch_shapes=[pltpu.SemaphoreType.DMA((2,))],
+        compiler_params=pltpu.CompilerParams(vmem_limit_bytes=1024 * 1024),
+        name="put_out",
+    )(state, marginal)
 
 
 def solution(mesh):

time: 72.4 us -> 71.8 us (level)
  local copies, waits for them, and re-layouts: 1.63 us -> 0 us
  Pallas kernels: 70 us -> 71 us
    unnamed x2 -> x0, local copies, waits for them, and re-layouts: 1.63 us -> none
    pallas_call x0 -> x1, Pallas kernels: none -> 1.02 us  [shards(): pl.pallas_call(put_out, out_shape=(jax.ShapeDtypeStruct(state.shape, f32)...]
where the time goes in v3:
time: 71.8 us; the launch traced here: 71.6 us
  Pallas kernels  71 us (99%)
    pallas_call x1, Pallas kernels, shards(): pl.pallas_call(functools.partial(kernel, n_bank, n_lane, chunks), out_sha...  70 us

profile of v3, /device:TPU:1, one launch (start us, length us, event | category | flops | bytes accessed | tf_op | source)
XLA Modules:
  0.0 71.6 jit_solution(15166180254858112888)
XLA Ops:
  0.6 70.0 %walsh.1 = (f32[2,8,128,128]{3,2,1,0:T(8,128)S(1)}, f32[8,32,128]{2,1,0:T(8,128)S(1)}) custom-call(f32[2,8,128,128]{3,2,1,0:T(8,128)} %a_hbm.1, f32[32,32,128]{2,1,0:T(8,128)} %bitcast.1, f32[2,128]{1,0:T(2,128)} %angle_hbm.1, bf16[256,256]{1,0:T(8,128)(2,1)} %constant.2.clone.table_hbm), custom_call_target="tpu_custom_call" | custom-call | tf_op jit(solution)/shard_map/walsh/pallas_call | solution.py:288
  70.6 1.0 %put_out.1 = (f32[2,8,128,128]{3,2,1,0:T(8,128)}, f32[8,32,128]{2,1,0:T(8,128)}) custom-call(f32[2,8,128,128]{3,2,1,0:T(8,128)S(1)} %get-tuple-element.4.state_ref, f32[8,32,128]{2,1,0:T(8,128)S(1)} %get-tuple-element.5.marginal_ref), custom_call_target="tpu_custom_call" | custom-call | tf_op jit(solution)/shard_map/put_out/pallas_call | solution.py:316
